TPU v7x, 256 devices: a whole 4x4x8 slice. The times are simulated.
256 devices in a mesh: dp: 32 (over x, z), frames: 8 (over y, core).
Axes of the slice: x: 4, y: 4, z: 8, core: 2. Of those that a mesh axis runs over, the one named last changes fastest.
Arguments:
- token_ids: int32 [128], P('dp'), may hold values from 0 to 26623
- positions: int32 [128], P('dp'), may hold values from 1 to 255
- embed: bfloat16 [26624, 1280], P(('dp', 'frames')), may hold values from -32 to 32
- pos_table: bfloat16 [256, 1280], replicated, may hold values from -4 to 4
- self_keys: bfloat16 [128, 256, 1280], P('dp', 'frames'), may hold values from -150 to 150
- self_values: bfloat16 [128, 256, 1280], P('dp', 'frames'), may hold values from -6 to 6
- cross_keys: bfloat16 [128, 512, 1280], P('dp', 'frames'), may hold values from -150 to 150
- cross_values: bfloat16 [128, 512, 1280], P('dp', 'frames'), may hold values from -6 to 6
- norm_gains: float32 [4, 1280], replicated, may hold values from 0.1 to 1.9
- qkv_weight: bfloat16 [3, 1280, 1280], P(None, None, 'frames'), may hold values from -0.15625 to 0.15625
- out_weight: bfloat16 [1280, 1280], P(None, 'frames'), may hold values from -0.15625 to 0.15625
- cross_query_weight: bfloat16 [1280, 1280], P(None, 'frames'), may hold values from -0.15625 to 0.15625
- cross_out_weight: bfloat16 [1280, 1280], P(None, 'frames'), may hold values from -0.15625 to 0.15625
- up_weight: bfloat16 [1280, 5120], P(None, 'frames'), may hold values from -0.15625 to 0.15625
- down_weight: bfloat16 [5120, 1280], P('frames'), may hold values from -0.078125 to 0.078125
Outputs:
- log_probs: float32 [128, 26624], P(None, ('dp', 'frames'))
Inputs may be any that keep to these rules, and one draw needn't show every extreme that they name: Stream s holds earlier tokens in cache slots 0 to positions[s] - 1; later slots are unused.
All inputs are finite; a program needn't handle non-finite values.
Results may differ from a plain program's by a relative error of at most 0.014.
Values may be sent and summed in bfloat16 or wider, within the bound.
A program may use at most 64 MiB of HBM per device.

v0:
```python
import jax
import jax.numpy as jnp
from jax import lax
from jax.sharding import Mesh
from jax.sharding import PartitionSpec as P

HEADS = 20
DP = ("dp_0", "dp_1")
FRAMES = ("frames_0", "frames_1")
DP_FRAMES = ("dp_0", "dp_1", "frames_0", "frames_1")


def copy_for_each(value, axis):
    devices = lax.axis_size(axis)
    return lax.all_to_all(
        jnp.broadcast_to(value[None], (devices, *value.shape)), axis, 0, 0, tiled=True
    )


def joined_along(blocks, dim):
    blocks = jnp.moveaxis(blocks, 0, dim)
    dims = blocks.shape
    return blocks.reshape(*dims[:dim], dims[dim] * dims[dim + 1], *dims[dim + 2 :])


def gathered_copies(value, axis, dim):
    blocks = copy_for_each(value, axis)
    return joined_along(blocks, dim)


def over_copies(value, axis):
    return copy_for_each(value, axis).sum(axis=0)


def all_in_one(value, axis):
    leaves = jax.tree.leaves(value)
    turns = sorted(range(len(leaves)), key=lambda k: -leaves[k].size)
    width = (1, *leaves[turns[0]].shape)[-1]
    lines = [
        jnp.pad(leaves[k].reshape(-1), (0, -leaves[k].size % width)).reshape(-1, width)
        for k in turns
    ]
    both, at, found = (copy_for_each(jnp.concatenate(lines), axis), 0, {})
    for k, line in zip(turns, lines):
        slab = both[:, at : at + len(line)].reshape(len(both), -1)
        found[k] = slab[:, : leaves[k].size].reshape(-1, *leaves[k].shape)
        at += len(line)
    numbers = iter(range(len(leaves)))
    return jax.tree.map(lambda _: found[next(numbers)], value)


def folded_in_pairs(pieces, combine):
    while len(jax.tree.leaves(pieces)[0]) > 1:
        pieces = jax.vmap(combine)(
            *(jax.tree.map(lambda part: part[side::2], pieces) for side in (0, 1))
        )
    return jax.tree.map(lambda part: part[0], pieces)


def combined_all(value, axis, combine):
    pieces = all_in_one(value, axis)
    return folded_in_pairs(pieces, combine)


def collected_together(value, axis):
    leaves = jax.tree.leaves(value)
    turns = sorted(range(len(leaves)), key=lambda k: -leaves[k].size)
    width = (1, *leaves[turns[0]].shape)[-1]
    lines = [
        jnp.pad(leaves[k].reshape(-1), (0, -leaves[k].size % width)).reshape(-1, width)
        for k in turns
    ]
    both, at, found = (lax.all_gather(jnp.concatenate(lines), axis), 0, {})
    for k, line in zip(turns, lines):
        slab = both[:, at : at + len(line)].reshape(len(both), -1)
        found[k] = slab[:, : leaves[k].size].reshape(-1, *leaves[k].shape)
        at += len(line)
    numbers = iter(range(len(leaves)))
    return jax.tree.map(lambda _: found[next(numbers)], value)


def joined_all(value, axes, combine):
    for axis in axes:
        pieces = collected_together(value, axis)
        value = jax.tree.map(lambda part: part[0], pieces)
        for k in range(1, lax.axis_size(axis)):
            value = combine(value, jax.tree.map(lambda part: part[k], pieces))
    return value


def layer_norm(values, gain):
    mean = jnp.mean(values, axis=-1, keepdims=True)
    centred = values - mean
    spread = jnp.mean(centred * centred, axis=-1, keepdims=True)
    return centred / jnp.sqrt(spread + 1e-05) * gain


def join_softmax(first, second):
    top = jnp.maximum(first[0], second[0])
    left = jnp.exp(first[0] - top)
    right = jnp.exp(second[0] - top)
    return (
        top,
        first[1] * left + second[1] * right,
        first[2] * left[..., None] + second[2] * right[..., None],
    )


def join_totals(first, second):
    top = jnp.maximum(first[0], second[0])
    return (top, first[1] * jnp.exp(first[0] - top) + second[1] * jnp.exp(second[0] - top))


def split_heads(values):
    return values.reshape(values.shape[0], HEADS, values.shape[1] // HEADS)


def partial_attention(query, keys, values, valid):
    streams, slots, width = keys.shape
    size = width // HEADS
    keys4 = keys.reshape(streams, slots, HEADS, size)
    vals4 = values.reshape(streams, slots, HEADS, size)
    scores = jnp.einsum(
        "she,sche->shc", query, keys4, preferred_element_type=jnp.float32
    ) * size ** (-0.5)
    masked = jnp.where(valid[:, None, :], scores, -1e30)
    peak = jnp.max(masked, axis=-1)
    weights = jnp.where(valid[:, None, :], jnp.exp(masked - peak[..., None]), 0.0)
    total = jnp.sum(weights, axis=-1)
    mixed = jnp.einsum(
        "shc,sche->she", weights.astype(jnp.bfloat16), vals4, preferred_element_type=jnp.float32
    )
    return (peak, total, mixed)


def on_device(
    token_ids,
    positions,
    embed,
    pos_table,
    self_keys,
    self_values,
    cross_keys,
    cross_values,
    norm_gains,
    qkv_weight,
    out_weight,
    cross_query_weight,
    cross_out_weight,
    up_weight,
    down_weight,
):
    streams = token_ids.shape[0]
    width = embed.shape[1]
    size = width // HEADS
    factor = jnp.float32(size) ** (-0.5)
    vocab_rows = embed.shape[0]
    shard = lax.axis_index(DP) * lax.axis_size(FRAMES) + lax.axis_index(FRAMES)
    all_ids = gathered_copies(token_ids, DP, 0)
    columns = shard * vocab_rows + jnp.arange(vocab_rows, dtype=jnp.int32)
    match = (all_ids[:, None] == columns[None, :]).astype(jnp.bfloat16)
    found = jnp.dot(match, embed, preferred_element_type=jnp.float32)
    blocks = lax.all_to_all(found.astype(jnp.bfloat16), DP, split_axis=0, concat_axis=0, tiled=True)
    local = jnp.sum(blocks.reshape(lax.axis_size(DP), streams, width).astype(jnp.float32), axis=0)
    tokens = over_copies(local, FRAMES)
    place_hit = (
        positions[:, None] == jnp.arange(pos_table.shape[0], dtype=jnp.int32)[None, :]
    ).astype(jnp.bfloat16)
    start = tokens + jnp.dot(place_hit, pos_table, preferred_element_type=jnp.float32)
    normed = layer_norm(start, norm_gains[0]).astype(jnp.bfloat16)
    qkv_local = jnp.einsum(
        "sd,jde->jse", normed, qkv_weight, preferred_element_type=jnp.float32
    ).astype(jnp.bfloat16)
    qkv = gathered_copies(qkv_local, FRAMES, 2)
    query, key_new, value_new = (split_heads(qkv[0]), split_heads(qkv[1]), split_heads(qkv[2]))
    slots = self_keys.shape[1]
    slot_index = lax.axis_index(FRAMES) * slots + jnp.arange(slots, dtype=jnp.int32)
    valid = slot_index[None, :] < positions[:, None]
    peak, total, mixed = combined_all(
        partial_attention(query, self_keys, self_values, valid), FRAMES, join_softmax
    )
    own = jnp.sum(query.astype(jnp.float32) * key_new.astype(jnp.float32), axis=-1) * factor
    top = jnp.maximum(peak, own)
    kept = jnp.exp(peak - top)
    own_weight = jnp.exp(own - top)
    total = total * kept + own_weight
    mixed = mixed * kept[..., None] + own_weight[..., None] * value_new.astype(jnp.float32)
    self_mix = (mixed / total[..., None]).reshape(streams, width).astype(jnp.bfloat16)
    self_part = jnp.dot(self_mix, out_weight, preferred_element_type=jnp.float32).astype(
        jnp.bfloat16
    )
    self_out = gathered_copies(self_part, FRAMES, 1)
    after_self = start + self_out.astype(jnp.float32)
    normed2 = layer_norm(after_self, norm_gains[1]).astype(jnp.bfloat16)
    cross_part = jnp.dot(normed2, cross_query_weight, preferred_element_type=jnp.float32).astype(
        jnp.bfloat16
    )
    cross_query = split_heads(gathered_copies(cross_part, FRAMES, 1))
    every_frame = jnp.ones((streams, cross_keys.shape[1]), dtype=bool)
    cpeak, ctotal, cmixed = combined_all(
        partial_attention(cross_query, cross_keys, cross_values, every_frame), FRAMES, join_softmax
    )
    cross_mix = (cmixed / ctotal[..., None]).reshape(streams, width).astype(jnp.bfloat16)
    cross_piece = jnp.dot(cross_mix, cross_out_weight, preferred_element_type=jnp.float32).astype(
        jnp.bfloat16
    )
    cross_out = gathered_copies(cross_piece, FRAMES, 1)
    after_cross = after_self + cross_out.astype(jnp.float32)
    normed3 = layer_norm(after_cross, norm_gains[2]).astype(jnp.bfloat16)
    hidden = jax.nn.gelu(
        jnp.dot(normed3, up_weight, preferred_element_type=jnp.float32), approximate=False
    ).astype(jnp.bfloat16)
    down_terms = jnp.dot(hidden, down_weight, preferred_element_type=jnp.float32)
    after_mlp = after_cross + over_copies(down_terms, FRAMES)
    final = layer_norm(after_mlp, norm_gains[3]).astype(jnp.bfloat16)
    logits = lax.dot_general(
        gathered_copies(final, DP, 0),
        embed,
        (((1,), (1,)), ((), ())),
        preferred_element_type=jnp.float32,
    )
    local_best = jnp.max(logits, axis=1)
    local_sum = jnp.sum(jnp.exp(logits - local_best[:, None]), axis=1)
    best, summed = joined_all((local_best, local_sum), DP_FRAMES, join_totals)
    return logits - best[:, None] - jnp.log(summed)[:, None]


def solution(mesh):
    finer = Mesh(mesh.devices.reshape(4, 8, 4, 2), ("dp_0", "dp_1", "frames_0", "frames_1"))
    in_specs = (
        P(DP),
        P(DP),
        P(DP_FRAMES, None),
        P(),
        P(DP, FRAMES, None),
        P(DP, FRAMES, None),
        P(DP, FRAMES, None),
        P(DP, FRAMES, None),
        P(),
        P(None, None, FRAMES),
        P(None, FRAMES),
        P(None, FRAMES),
        P(None, FRAMES),
        P(None, FRAMES),
        P(FRAMES, None),
    )
    out_specs = P(None, DP_FRAMES)
    return jax.shard_map(
        on_device, mesh=finer, in_specs=in_specs, out_specs=out_specs, check_vma=False
    )
```

profile of v0, /device:TPU:1, one launch (start us, length us, event | category | flops | bytes accessed | tf_op | source)
XLA Modules:
  0.0 203.0 jit_solution(1766089785197812769)
XLA Ops:
  0.0 1.4 broadcast_in_dim.46
  1.4 11.9 %all-to-all-start = ((s32[32,1,4]{2,1,0:T(1,128)}), s32[32,1,4]{2,1,0:T(1,128)S(1)}, u32[]{:S(2)}, u32[]{:S(2)}) async-start(s32[32,1,4]{2,1,0:T(1,128)} %broadcast_in_dim.46), calls=%async_computation | async-start | bytes 32768 | tf_op jit(solution)/shard_map/all_to_all | solution.py:15
  13.3 8.6 %all-to-all-done = s32[32,1,4]{2,1,0:T(1,128)S(1)} async-done(((s32[32,1,4]{2,1,0:T(1,128)}), s32[32,1,4]{2,1,0:T(1,128)S(1)}, u32[]{:S(2)}, u32[]{:S(2)}) %all-to-all-start) | async-done | bytes 544 | tf_op jit(solution)/shard_map/all_to_all | solution.py:15
  22.4 0.7 reduce.15
  23.2 1.2 convolution_convert_fusion
  24.4 0.8 all_to_all.38
  25.2 3.9 %all-to-all-start.1 = ((bf16[32,4,1280]{2,1,0:T(4,128)(2,1)}), bf16[32,4,1280]{2,1,0:T(4,128)(2,1)S(1)}, u32[]{:S(2)}, u32[]{:S(2)}) async-start(bf16[32,4,1280]{2,1,0:T(4,128)(2,1)} %all_to_all.38), calls=%async_computation.1 | async-start | bytes 655360 | tf_op jit(solution)/shard_map/all_to_all | solution.py:163
  29.1 9.9 %all-to-all-done.1 = bf16[32,4,1280]{2,1,0:T(4,128)(2,1)S(1)} async-done(((bf16[32,4,1280]{2,1,0:T(4,128)(2,1)}), bf16[32,4,1280]{2,1,0:T(4,128)(2,1)S(1)}, u32[]{:S(2)}, u32[]{:S(2)}) %all-to-all-start.1) | async-done | bytes 327712 | tf_op jit(solution)/shard_map/all_to_all | solution.py:163
  39.9 9.0 %all-to-all-start.2 = ((f32[8,4,1280]{2,1,0:T(4,128)}), f32[8,4,1280]{2,1,0:T(4,128)S(1)}, u32[]{:S(2)}, u32[]{:S(2)}) async-start(f32[8,4,1280]{2,1,0:T(4,128)} %broadcast_in_dim.47), calls=%async_computation.2 | async-start | bytes 327680 | tf_op jit(solution)/shard_map/all_to_all | solution.py:15
  48.8 1.5 slice_reduce_fusion
  50.4 4.0 %all-to-all-done.2 = f32[8,4,1280]{2,1,0:T(4,128)S(1)} async-done(((f32[8,4,1280]{2,1,0:T(4,128)}), f32[8,4,1280]{2,1,0:T(4,128)S(1)}, u32[]{:S(2)}, u32[]{:S(2)}) %all-to-all-start.2) | async-done | bytes 163872 | tf_op jit(solution)/shard_map/all_to_all | solution.py:15
  54.4 1.4 fusion.188
  57.2 4.8 %all-to-all-start.3 = ((bf16[8,3,4,160]{3,2,1,0:T(4,128)(2,1)}), bf16[8,3,4,160]{3,2,1,0:T(4,128)(2,1)}, u32[]{:S(2)}, u32[]{:S(2)}) async-start(bf16[8,3,4,160]{3,2,1,0:T(4,128)(2,1)} %broadcast_in_dim.49), calls=%async_computation.3 | async-start | bytes 98304 | tf_op jit(solution)/shard_map/all_to_all | solution.py:15
  62.6 1.5 reshape.1081
  64.1 2.8 %all-to-all-done.3 = bf16[8,3,4,160]{3,2,1,0:T(4,128)(2,1)} async-done(((bf16[8,3,4,160]{3,2,1,0:T(4,128)(2,1)}), bf16[8,3,4,160]{3,2,1,0:T(4,128)(2,1)}, u32[]{:S(2)}, u32[]{:S(2)}) %all-to-all-start.3) | async-done | bytes 30752 | tf_op jit(solution)/shard_map/all_to_all | solution.py:15
  66.9 0.8 copy.186
  69.5 0.7 broadcast_in_dim.52
  70.2 4.1 %all-to-all-start.4 = ((f32[8,84,64]{1,2,0:T(8,128)}), f32[8,84,64]{1,2,0:T(8,128)S(1)}, u32[]{:S(2)}, u32[]{:S(2)}) async-start(f32[8,84,64]{1,2,0:T(8,128)} %broadcast_in_dim.52), calls=%async_computation.4 | async-start | bytes 524288 | tf_op jit(solution)/shard_map/all_to_all | solution.py:15
  74.7 6.1 %all-to-all-done.4 = f32[8,84,64]{1,2,0:T(8,128)S(1)} async-done(((f32[8,84,64]{1,2,0:T(8,128)}), f32[8,84,64]{1,2,0:T(8,128)S(1)}, u32[]{:S(2)}, u32[]{:S(2)}) %all-to-all-start.4) | async-done | bytes 172064 | tf_op jit(solution)/shard_map/all_to_all | solution.py:15
  84.8 8.0 %all_to_all.60 = bf16[8,4,160]{2,1,0:T(4,128)(2,1)S(1)} all-to-all(bf16[8,4,160]{2,1,0:T(4,128)(2,1)S(1)} %broadcast_in_dim.53), channel_id=1, replica_groups=mesh['dp_0'=4,'dp_1'=8,'frames_0'=4,'frames_1'=2] {'frames_0','frames_1'}, dimensions={0} | all-to-all | bytes 20480 | tf_op jit(solution)/shard_map/all_to_all | solution.py:15
  93.3 1.2 convolution_convert_fusion.3
  94.5 0.7 broadcast_in_dim.54
  95.2 3.9 %all-to-all-start.6 = ((bf16[8,4,160]{2,1,0:T(4,128)(2,1)}), bf16[8,4,160]{2,1,0:T(4,128)(2,1)S(1)}, u32[]{:S(2)}, u32[]{:S(2)}) async-start(bf16[8,4,160]{2,1,0:T(4,128)(2,1)} %broadcast_in_dim.54), calls=%async_computation.6 | async-start | bytes 32768 | tf_op jit(solution)/shard_map/all_to_all | solution.py:15
  99.2 1.4 copy.150
  100.6 2.1 %reshape.1092 = bf16[4,64,20,64]{3,2,1,0:T(8,128)(2,1)S(1)} reshape(bf16[4,64,1280]{2,1,0:T(8,128)(2,1)} %param.22) | data formatting | bytes 1310720 | tf_op jit(solution)/shard_map/reshape | solution.py:122
  102.7 1.2 all-to-all-done.6
  103.9 1.8 fusion.190
  107.1 9.9 %all_to_all.61 = f32[8,84,64]{1,2,0:T(8,128)S(1)} all-to-all(f32[8,84,64]{1,2,0:T(8,128)S(1)} %broadcast_in_dim.55), channel_id=1, replica_groups=mesh['dp_0'=4,'dp_1'=8,'frames_0'=4,'frames_1'=2] {'frames_0','frames_1'}, dimensions={0} | all-to-all | bytes 344064 | tf_op jit(solution)/shard_map/all_to_all | solution.py:15
  117.2 1.3 slice.396
  118.6 1.3 slice.391
  120.1 0.7 copy.130
  120.8 0.9 reshape.1098
  121.7 0.7 copy.135
  122.5 0.8 reshape.1100
  124.2 1.2 multiply_add_fusion
  125.7 1.3 slice.397
  127.0 0.7 multiply_add_fusion.6
  128.1 0.7 copy.134
  128.8 1.1 multiply_add_fusion.2
  130.3 1.2 convolution_convert_fusion.2
  131.5 8.0 %all_to_all.62 = bf16[8,4,160]{2,1,0:T(4,128)(2,1)S(1)} all-to-all(bf16[8,4,160]{2,1,0:T(4,128)(2,1)S(1)} %broadcast_in_dim.56), channel_id=1, replica_groups=mesh['dp_0'=4,'dp_1'=8,'frames_0'=4,'frames_1'=2] {'frames_0','frames_1'}, dimensions={0} | all-to-all | bytes 20480 | tf_op jit(solution)/shard_map/all_to_all | solution.py:15
  140.0 0.7 fusion.46
  140.8 8.8 %all_to_all.63 = f32[8,4,1280]{2,1,0:T(4,128)S(1)} all-to-all(f32[8,4,1280]{2,1,0:T(4,128)S(1)} %broadcast_in_dim.61), channel_id=1, replica_groups=mesh['dp_0'=4,'dp_1'=8,'frames_0'=4,'frames_1'=2] {'frames_0','frames_1'}, dimensions={0} | all-to-all | bytes 327680 | tf_op jit(solution)/shard_map/all_to_all | solution.py:15
  150.1 14.3 %all_to_all.64 = bf16[32,4,1280]{2,1,0:T(4,128)(2,1)S(1)} all-to-all(bf16[32,4,1280]{2,1,0:T(4,128)(2,1)S(1)} %broadcast_in_dim.62), channel_id=1, replica_groups=mesh['dp_0'=4,'dp_1'=8,'frames_0'=4,'frames_1'=2] {'dp_0','dp_1'}, dimensions={0} | all-to-all | bytes 655360 | tf_op jit(solution)/shard_map/all_to_all | solution.py:15
  164.8 6.9 %all-gather.4 = f32[4,2,128]{2,1,0:T(2,128)S(1)} all-gather(f32[1,2,128]{2,1,0:T(2,128)S(1)} %maximum_bitcast_fusion), channel_id=2, replica_groups=mesh['dp_0'=4,'dp_1'=8,'frames_0'=4,'frames_1'=2] {'dp_0'}, dimensions={0}, use_global_device_ids=true | all-gather | bytes 5120 | tf_op jit(solution)/shard_map/all_gather | solution.py:73
  171.7 13.0 %all-gather.5 = f32[8,2,128]{2,1,0:T(2,128)S(1)} all-gather(f32[1,2,128]{2,1,0:T(2,128)S(1)} %maximum_bitcast_fusion.1), channel_id=3, replica_groups=mesh['dp_0'=4,'dp_1'=8,'frames_0'=4,'frames_1'=2] {'dp_1'}, dimensions={0}, use_global_device_ids=true | all-gather | bytes 9216 | tf_op jit(solution)/shard_map/all_gather | solution.py:73
  184.7 6.1 %all-gather.6 = f32[4,2,128]{2,1,0:T(2,128)S(1)} all-gather(f32[1,2,128]{2,1,0:T(2,128)S(1)} %maximum_bitcast_fusion.2), channel_id=4, replica_groups=mesh['dp_0'=4,'dp_1'=8,'frames_0'=4,'frames_1'=2] {'frames_0'}, dimensions={0}, use_global_device_ids=true | all-gather | bytes 5120 | tf_op jit(solution)/shard_map/all_gather | solution.py:73
  190.9 11.4 %all-gather.7 = f32[2,2,128]{2,1,0:T(2,128)S(1)} all-gather(f32[1,2,128]{2,1,0:T(2,128)S(1)} %maximum_bitcast_fusion.3), channel_id=5, replica_groups=mesh['dp_0'=4,'dp_1'=8,'frames_0'=4,'frames_1'=2] {'frames_1'}, dimensions={0}, use_global_device_ids=true | all-gather | bytes 3072 | tf_op jit(solution)/shard_map/all_gather | solution.py:73
  (164 shorter events, 15.8 us)
Async XLA Ops:
  0.0 140.0 %copy-start = (bf16[640,1280]{1,0:T(8,128)(2,1)S(1)}, bf16[640,1280]{1,0:T(8,128)(2,1)}, u32[]{:S(2)}) copy-start(bf16[640,1280]{1,0:T(8,128)(2,1)} %param.29) | copy-start | bytes 4915204
  0.0 54.4 %copy-start.13 = (s32[4]{0:T(128)S(1)}, s32[4]{0:T(128)}, u32[]{:S(2)}) copy-start(s32[4]{0:T(128)} %param.16) | copy-start | bytes 52
  1.4 20.5 %all-to-all-start = ((s32[32,1,4]{2,1,0:T(1,128)}), s32[32,1,4]{2,1,0:T(1,128)S(1)}, u32[]{:S(2)}, u32[]{:S(2)}) async-start(s32[32,1,4]{2,1,0:T(1,128)} %broadcast_in_dim.46), calls=%async_computation | async-start | bytes 32768 | tf_op jit(solution)/shard_map/all_to_all | solution.py:15
  24.4 31.7 %copy-start.2 = (bf16[3,1280,160]{1,2,0:T(8,128)(2,1)S(1)}, bf16[3,1280,160]{1,2,0:T(8,128)(2,1)}, u32[]{:S(2)}) copy-start(bf16[3,1280,160]{1,2,0:T(8,128)(2,1)} %param.24) | copy-start | bytes 3686404
  25.2 13.8 %all-to-all-start.1 = ((bf16[32,4,1280]{2,1,0:T(4,128)(2,1)}), bf16[32,4,1280]{2,1,0:T(4,128)(2,1)S(1)}, u32[]{:S(2)}, u32[]{:S(2)}) async-start(bf16[32,4,1280]{2,1,0:T(4,128)(2,1)} %all_to_all.38), calls=%async_computation.1 | async-start | bytes 655360 | tf_op jit(solution)/shard_map/all_to_all | solution.py:163
  29.1 33.0 %copy-start.6 = (bf16[4,32,1280]{2,1,0:T(8,128)(2,1)S(1)}, bf16[4,32,1280]{2,1,0:T(8,128)(2,1)}, u32[]{:S(2)}) copy-start(bf16[4,32,1280]{2,1,0:T(8,128)(2,1)} %param.19) | copy-start | bytes 983044
  39.9 14.5 %all-to-all-start.2 = ((f32[8,4,1280]{2,1,0:T(4,128)}), f32[8,4,1280]{2,1,0:T(4,128)S(1)}, u32[]{:S(2)}, u32[]{:S(2)}) async-start(f32[8,4,1280]{2,1,0:T(4,128)} %broadcast_in_dim.47), calls=%async_computation.2 | async-start | bytes 327680 | tf_op jit(solution)/shard_map/all_to_all | solution.py:15
  55.9 6.1 %copy-start.7 = (f32[4,1280]{1,0:T(4,128)}, f32[4,1280]{1,0:T(4,128)S(1)}, u32[]{:S(2)}) copy-start(f32[4,1280]{1,0:T(4,128)S(1)} %get-tuple-element.60) | copy-start | bytes 61444
  57.2 9.7 %all-to-all-start.3 = ((bf16[8,3,4,160]{3,2,1,0:T(4,128)(2,1)}), bf16[8,3,4,160]{3,2,1,0:T(4,128)(2,1)}, u32[]{:S(2)}, u32[]{:S(2)}) async-start(bf16[8,3,4,160]{3,2,1,0:T(4,128)(2,1)} %broadcast_in_dim.49), calls=%async_computation.3 | async-start | bytes 98304 | tf_op jit(solution)/shard_map/all_to_all | solution.py:15
  70.2 10.6 %all-to-all-start.4 = ((f32[8,84,64]{1,2,0:T(8,128)}), f32[8,84,64]{1,2,0:T(8,128)S(1)}, u32[]{:S(2)}, u32[]{:S(2)}) async-start(f32[8,84,64]{1,2,0:T(8,128)} %broadcast_in_dim.52), calls=%async_computation.4 | async-start | bytes 524288 | tf_op jit(solution)/shard_map/all_to_all | solution.py:15
  81.6 2.9 %copy-start.5 = (bf16[1280,160]{0,1:T(8,128)(2,1)S(1)}, bf16[1280,160]{0,1:T(8,128)(2,1)}, u32[]{:S(2)}) copy-start(bf16[1280,160]{0,1:T(8,128)(2,1)} %param.25) | copy-start | bytes 1228804
  81.8 11.1 %copy-start.8 = (f32[4,1280]{1,0:T(4,128)S(1)}, f32[4,1280]{1,0:T(4,128)}, u32[]{:S(2)}) copy-start(f32[4,1280]{1,0:T(4,128)} %copy-done.7) | copy-start | bytes 61444
  82.0 11.3 %copy-start.12 = (f32[1280]{0:T(1024)S(1)}, f32[1280]{0:T(1024)}, u32[]{:S(2)}) copy-start(f32[1280]{0:T(1024)} %get-tuple-element.6) | copy-start | bytes 15364
  82.5 16.7 %copy-start.4 = (bf16[4,64,1280]{2,1,0:T(8,128)(2,1)S(1)}, bf16[4,64,1280]{2,1,0:T(8,128)(2,1)}, u32[]{:S(2)}) copy-start(bf16[4,64,1280]{2,1,0:T(8,128)(2,1)} %param.21) | copy-start | bytes 1966084
  93.1 6.1 %copy-start.9 = (f32[4,1280]{1,0:T(4,128)}, f32[4,1280]{1,0:T(4,128)S(1)}, u32[]{:S(2)}) copy-start(f32[4,1280]{1,0:T(4,128)S(1)} %get-tuple-element.30) | copy-start | bytes 61444
  95.2 8.6 %all-to-all-start.6 = ((bf16[8,4,160]{2,1,0:T(4,128)(2,1)}), bf16[8,4,160]{2,1,0:T(4,128)(2,1)S(1)}, u32[]{:S(2)}, u32[]{:S(2)}) async-start(bf16[8,4,160]{2,1,0:T(4,128)(2,1)} %broadcast_in_dim.54), calls=%async_computation.6 | async-start | bytes 32768 | tf_op jit(solution)/shard_map/all_to_all | solution.py:15
  120.8 19.2 %copy-start.1 = (bf16[1280,640]{1,0:T(8,128)(2,1)S(1)}, bf16[1280,640]{1,0:T(8,128)(2,1)}, u32[]{:S(2)}) copy-start(bf16[1280,640]{1,0:T(8,128)(2,1)} %param.28) | copy-start | bytes 4915204
  125.5 14.2 %copy-start.10 = (f32[4,1280]{1,0:T(4,128)S(1)}, f32[4,1280]{1,0:T(4,128)}, u32[]{:S(2)}) copy-start(f32[4,1280]{1,0:T(4,128)} %copy-done.9) | copy-start | bytes 61444
  140.0 9.9 %copy-start.11 = (f32[1280]{0:T(1024)S(1)}, f32[1280]{0:T(1024)}, u32[]{:S(2)}) copy-start(f32[1280]{0:T(1024)} %get-tuple-element.5) | copy-start | bytes 15364
  140.8 23.7 %copy-start.3 = (bf16[104,1280]{1,0:T(8,128)(2,1)S(1)}, bf16[104,1280]{1,0:T(8,128)(2,1)}, u32[]{:S(2)}) copy-start(bf16[104,1280]{1,0:T(8,128)(2,1)} %param.17) | copy-start | bytes 798724
where the time goes:
time: 204 us; the launch traced here: 203 us
  blocking collectives  86.5 us (42%)
  starting transfers between devices  37.5 us (18%)
  waiting for transfers between devices  32.6 us (16%)
  local copies, waits for them, and re-layouts  27.8 us (14%)
  matrix products  9.54 us (5%)
  other arithmetic  8.54 us (4%)
    all_to_all x5, blocking collectives, copy_for_each(): lax.all_to_all(jnp.broadcast_to(value[None], (devices, *value.shape)), ax...  49.1 us
    all_gather x4, blocking collectives, collected_together(): both, at, found = (lax.all_gather(jnp.concatenate(lines), axis), 0, {})  37.4 us
    all_to_all x5, starting transfers between devices, copy_for_each(): lax.all_to_all(jnp.broadcast_to(value[None], (devices, *value.shape)), ax...  33.6 us
    all_to_all x5, waiting for transfers between devices, copy_for_each(): lax.all_to_all(jnp.broadcast_to(value[None], (devices, *value.shape)), ax...  22.7 us
    all_to_all x1, waiting for transfers between devices, on_device(): lax.all_to_all(found.astype(jnp.bfloat16), DP, split_axis=0, concat_axis=...  9.93 us
    slice x8, local copies, waits for them, and re-layouts, folded_in_pairs(): part[side::2]  5.03 us
    broadcast_in_dim x10, local copies, waits for them, and re-layouts, copy_for_each(): jnp.broadcast_to(value[None], (devices, *value.shape))  4.47 us
  transfers between devices with their start and end apart: 6, of which 6 were waited for; matrix products, arithmetic and copies ran while one was open for 4% of the time, Pallas kernels for 0%

commit v1 on v0

v1 whole, which is shorter than its diff:
```python
import functools

import jax
import jax.numpy as jnp
from jax import lax
from jax.experimental import pallas as pl
from jax.experimental.pallas import tpu as pltpu
from jax.sharding import PartitionSpec as P

MESH = pl.DeviceIdType.MESH
F32, BF16, I32 = jnp.float32, jnp.bfloat16, jnp.int32
HEADS = 20
WIDTH = 1280
TILES = WIDTH // 128
NF = 8
PIECE = WIDTH // NF
NEG = -1e30
FIRST_TILE = [PIECE * k // 128 for k in range(NF)]


def nt(a, b):
    return lax.dot_general(a, b, (((1,), (1,)), ((), ())), preferred_element_type=F32)


def nn(a, b):
    return jnp.dot(a, b, preferred_element_type=F32)


def kernel(nd, vocab, slots, frames, hidden,
           tok_ref, pos_ref, emb_h, post_h, sk_h, sv_h, ck_h, cv_h, gain_h, qkv_h, ow_h, cqw_h, cow_h, up_h, down_h,
           out_ref,
           emb, post, sk, sv, ck, cv, gain, qkvw, ow, cqw, cow, up, down,
           pqkv, pow_, pcq, pco,
           ids_buf, ew, row_send, row_buf, tok_buf, qkv_buf, smix, sstat, so_buf, cq_buf, cmix, cstat, co_buf, dn_buf,
           fin_buf, st1, st2,
           lsem, ssem, rsem):
    d = lax.axis_index("dp")
    f = lax.axis_index("frames")
    sub = lax.broadcasted_iota(I32, (8, 128), 0)
    lane = lax.broadcasted_iota(I32, (8, 128), 1)
    low = sub < 4
    own_half = (sub // 4) == (lane // 64)

    def roll4(v):
        return pltpu.roll(v, 4, v.ndim - 2)

    pairs = [(emb_h, emb), (post_h, post), (qkv_h, qkvw), (gain_h, gain), (sk_h, sk), (sv_h, sv), (ow_h, ow),
             (cqw_h, cqw), (ck_h, ck), (cv_h, cv), (cow_h, cow), (up_h, up), (down_h, down)]
    local = {}
    for n, (src, dst) in enumerate(pairs):
        local[n] = pltpu.make_async_copy(src, dst, lsem.at[n])
        local[n].start()
    EMB, POST, QKV, GAIN, SK, SV, OW, CQW, CK, CV, COW, UP, DOWN = range(13)

    barrier = pltpu.get_barrier_semaphore()
    for k in range(1, nd):
        pl.semaphore_signal(barrier, inc=1, device_id=(lax.rem(d + k, nd), f), device_id_type=MESH)
    for k in range(1, NF):
        pl.semaphore_signal(barrier, inc=1, device_id=(d, lax.rem(f + k, NF)), device_id_type=MESH)

    exchanges = []

    def frames_send(n, buf):
        for k in range(1, NF):
            pltpu.make_async_remote_copy(
                src_ref=buf.at[f], dst_ref=buf.at[f], send_sem=ssem.at[n], recv_sem=rsem.at[n],
                device_id=(d, lax.rem(f + k, NF)), device_id_type=MESH).start()
        exchanges.append((n, buf, NF - 1))

    def dp_send(n, buf):
        for k in range(1, nd):
            pltpu.make_async_remote_copy(
                src_ref=buf.at[d], dst_ref=buf.at[d], send_sem=ssem.at[n], recv_sem=rsem.at[n],
                device_id=(lax.rem(d + k, nd), f), device_id_type=MESH).start()
        exchanges.append((n, buf, nd - 1))

    def received(n, buf, count):
        pltpu.make_async_copy(buf.at[pl.ds(0, count)], buf.at[pl.ds(0, count)], rsem.at[n]).wait()

    t0, t1, t2, t3 = (tok_ref[s] for s in range(4))
    p0, p1, p2, p3 = (pos_ref[s] for s in range(4))

    def by_stream(index, a, b, c, e):
        return jnp.where(index == 0, a, jnp.where(index == 1, b, jnp.where(index == 2, c, e)))

    ids_buf[d] = by_stream(sub % 4, t0, t1, t2, t3)
    pl.semaphore_wait(barrier, nd - 1 + NF - 1)
    dp_send(0, ids_buf)

    def first_lane(index):
        return pl.multiple_of(lax.div(index * 5, 4) * 128, 128)

    local[EMB].wait()
    for k in range(1, NF):
        peer = lax.rem(f + k, NF)
        pltpu.make_async_remote_copy(
            src_ref=emb.at[:, pl.ds(first_lane(peer), 256)], dst_ref=ew.at[f], send_sem=ssem.at[1], recv_sem=rsem.at[1],
            device_id=(d, peer), device_id_type=MESH).start()
    exchanges.append((1, ew, NF - 1))
    ew[f] = emb[:, pl.ds(first_lane(f), 256)]

    local[POST].wait()
    places = post.shape[0]
    place_at = by_stream(lax.broadcasted_iota(I32, (8, places), 0) % 4, p0, p1, p2, p3)
    place_hit = (lax.broadcasted_iota(I32, (8, places), 1) == place_at).astype(F32).astype(BF16)
    place = nn(place_hit, post[...])

    shift = lax.rem(f, 4) * 32
    move = (lax.broadcasted_iota(I32, (PIECE, 256), 1)
            == lax.broadcasted_iota(I32, (PIECE, 256), 0) + shift).astype(F32).astype(BF16)
    local[QKV].wait()
    for j in range(3):
        pqkv[j] = nn(qkvw[j], move).astype(BF16)
    local[OW].wait()
    pow_[...] = nn(ow[...], move).astype(BF16)
    local[CQW].wait()
    pcq[...] = nn(cqw[...], move).astype(BF16)
    local[COW].wait()
    pco[...] = nn(cow[...], move).astype(BF16)

    received(1, ew, NF - 1)
    received(0, ids_buf, nd - 1)
    ids = ids_buf[...].reshape(nd * 8, 128)[:, :vocab]
    row_of = lax.broadcasted_iota(I32, (nd * 8, vocab), 1)
    found = None
    for j in range(NF):
        hit = (ids == row_of + (d * NF + j) * vocab).astype(F32).astype(BF16)
        part = nn(hit, ew[j])
        found = part if found is None else found + part
    low_rows = (lax.broadcasted_iota(I32, (nd * 8, 128), 0) % 8) < 4
    folded = jnp.where(low_rows, found[:, :128], found[:, 128:])
    row_send[...] = folded.reshape(nd, 8, 128).astype(BF16)
    for k in range(1, nd):
        peer = lax.rem(d + k, nd)
        pltpu.make_async_remote_copy(
            src_ref=row_send.at[peer], dst_ref=row_buf.at[d], send_sem=ssem.at[2], recv_sem=rsem.at[2],
            device_id=(peer, f), device_id_type=MESH).start()
    exchanges.append((2, row_buf, nd - 1))
    row_buf[d] = row_send[d]
    received(2, row_buf, nd - 1)
    tok_buf[f] = jnp.sum(row_buf[...].astype(F32), axis=0).astype(BF16)
    frames_send(3, tok_buf)
    local[GAIN].wait()
    received(3, tok_buf, NF - 1)

    def unfold(v):
        other = roll4(v)
        return jnp.where(low, v, other), jnp.where(low, other, v)

    tiles = [None] * TILES
    for k in range(NF):
        first, second = unfold(tok_buf[k].astype(F32))
        tiles[FIRST_TILE[k]] = first
        if tiles[FIRST_TILE[k] + 1] is None:
            tiles[FIRST_TILE[k] + 1] = second
    start = jnp.concatenate(tiles, axis=1) + place

    def norm(values, row):
        mean = jnp.sum(values, axis=1, keepdims=True) * (1.0 / WIDTH)
        centred = values - mean
        spread = jnp.sum(centred * centred, axis=1, keepdims=True) * (1.0 / WIDTH)
        return (centred * lax.rsqrt(spread + 1e-5) * gain[row : row + 1, :]).astype(BF16)

    def fold_window(v):
        return jnp.where(low, v[:, :128], v[:, 128:]).astype(BF16)

    def columns_joined(pieces):
        tiles = [None] * TILES
        for k in range(NF):
            for at, part in zip((FIRST_TILE[k], FIRST_TILE[k] + 1), unfold(pieces[k].astype(F32))):
                tiles[at] = part if tiles[at] is None else tiles[at] + part
        return tiles

    normed = norm(start, 0)
    qkv_buf[f] = jnp.stack([fold_window(nn(normed, pqkv[j])) for j in range(3)])
    frames_send(4, qkv_buf)

    rows_r = 4 * HEADS

    def attend(query, key_ref, value_ref, count, valid, own):
        zero = jnp.zeros((8, 128), F32)
        blocks = []
        for t in range(TILES):
            block = [zero] * TILES
            block[t] = jnp.where(own_half, query[t], 0.0)
            blocks.append(jnp.concatenate(block, axis=1))
        spread_query = jnp.concatenate(blocks, axis=0).astype(BF16)
        keys = key_ref[...].reshape(4 * count, WIDTH)
        values = value_ref[...].reshape(4 * count, WIDTH)
        scores = nt(spread_query, keys) * 0.125
        scores = jnp.where(valid, scores, NEG)
        peak = jnp.max(scores, axis=1, keepdims=True)
        if own is not None:
            own_score = jnp.concatenate(own[0], axis=0)
            peak = jnp.maximum(peak, own_score)
        weights = jnp.where(valid, jnp.exp(scores - peak), 0.0)
        total = jnp.sum(weights, axis=1, keepdims=True)
        if own is not None:
            own_weight = jnp.where(own_score > 0.5 * NEG, jnp.exp(own_score - peak), 0.0)
            total = total + own_weight
        some = total > 0.0
        inverse = jnp.where(some, 1.0 / jnp.where(some, total, 1.0), 0.0)
        level = jnp.where(some, peak + jnp.log(jnp.where(some, total, 1.0)), NEG)
        stat = jnp.zeros((8, 128), F32)
        raw = []
        for t in range(TILES):
            at = slice(8 * t, 8 * t + 8)
            mixed = nn(weights[at].astype(BF16), values[:, 128 * t : 128 * t + 128])
            if own is not None:
                mixed = mixed + own_weight[at] * own[1][t]
            raw.append(mixed * inverse[at])
            stat = jnp.where(lane == t, level[at], stat)
        half = TILES // 2
        mix = [jnp.where(own_half, raw[t], roll4(raw[t + half])).astype(BF16) for t in range(half)]
        return jnp.stack(mix), stat

    def joined(mix_buf, stat_buf):
        levels = [stat_buf[k] for k in range(NF)]
        top = functools.reduce(jnp.maximum, levels)
        shares = [jnp.exp(v - top) for v in levels]
        inverse = 1.0 / functools.reduce(jnp.add, shares)
        shares = [v * inverse for v in shares]
        turned = [roll4(v) for v in shares]
        half = TILES // 2
        first, second = [], []
        for t in range(half):
            total = None
            for k in range(NF):
                share = jnp.where(own_half, jnp.broadcast_to(shares[k][:, t : t + 1], (8, 128)),
                                  jnp.broadcast_to(turned[k][:, t + half : t + half + 1], (8, 128)))
                term = share * mix_buf[k, t].astype(F32)
                total = term if total is None else total + term
            other = roll4(total)
            first.append(jnp.where(own_half, total, other))
            second.append(jnp.where(own_half, other, total))
        return jnp.concatenate(first + second, axis=1).astype(BF16)

    column = lax.broadcasted_iota(I32, (rows_r, 4 * slots), 1)
    same = (lax.broadcasted_iota(I32, (rows_r, 4 * slots), 0) % 4) == column // slots
    here = by_stream(column // slots, p0, p1, p2, p3)
    valid = jnp.logical_and(same, f * slots + column % slots < here)
    column = lax.broadcasted_iota(I32, (rows_r, 4 * frames), 1)
    every = (lax.broadcasted_iota(I32, (rows_r, 4 * frames), 0) % 4) == column // frames

    local[SK].wait()
    local[SV].wait()
    received(4, qkv_buf, NF - 1)
    query, key_new, value_new = (columns_joined([qkv_buf[k, j] for k in range(NF)]) for j in range(3))
    first_device = f == 0
    own_scores = []
    for t in range(TILES):
        score = jnp.sum(jnp.where(own_half, query[t] * key_new[t], 0.0), axis=1, keepdims=True) * 0.125
        own_scores.append(jnp.where(first_device, score, NEG))
    smix[f], sstat[f] = attend(query, sk, sv, slots, valid, (own_scores, value_new))
    frames_send(5, sstat)
    frames_send(6, smix)
    received(5, sstat, NF - 1)
    received(6, smix, NF - 1)
    self_mix = joined(smix, sstat)

    so_buf[f] = fold_window(nn(self_mix, pow_[...]))
    frames_send(7, so_buf)
    received(7, so_buf, NF - 1)
    after_self = start + jnp.concatenate(columns_joined([so_buf[k] for k in range(NF)]), axis=1)
    normed2 = norm(after_self, 1)
    cq_buf[f] = fold_window(nn(normed2, pcq[...]))
    frames_send(8, cq_buf)
    local[CK].wait()
    local[CV].wait()
    received(8, cq_buf, NF - 1)
    cross_query = columns_joined([cq_buf[k] for k in range(NF)])
    cmix[f], cstat[f] = attend(cross_query, ck, cv, frames, every, None)
    frames_send(9, cstat)
    frames_send(10, cmix)
    received(9, cstat, NF - 1)
    received(10, cmix, NF - 1)
    cross_mix = joined(cmix, cstat)
    co_buf[f] = fold_window(nn(cross_mix, pco[...]))
    frames_send(11, co_buf)
    local[UP].wait()
    local[DOWN].wait()
    received(11, co_buf, NF - 1)
    after_cross = after_self + jnp.concatenate(columns_joined([co_buf[k] for k in range(NF)]), axis=1)

    normed3 = norm(after_cross, 2)
    raised = nn(normed3, up[...])
    active = (raised * (1.0 + lax.erf(raised * (0.5 ** 0.5))) * 0.5).astype(BF16)
    lowered = nn(active, down[...])
    half = TILES // 2

    def tile(v, t):
        return v[:, 128 * t : 128 * t + 128]

    dn_buf[f] = jnp.stack([jnp.where(low, tile(lowered, t), tile(lowered, t + half)).astype(BF16) for t in range(half)])
    frames_send(12, dn_buf)
    received(12, dn_buf, NF - 1)
    summed = jnp.sum(dn_buf[...].astype(F32), axis=0)
    halves = [unfold(summed[t]) for t in range(half)]
    after_mlp = after_cross + jnp.concatenate([a for a, _ in halves] + [b for _, b in halves], axis=1)
    final = norm(after_mlp, 3).astype(F32)
    fin_buf[d] = jnp.stack([jnp.where(low, tile(final, t), tile(final, t + half)).astype(BF16) for t in range(half)])
    dp_send(13, fin_buf)
    received(13, fin_buf, nd - 1)

    low3 = lax.broadcasted_iota(I32, (nd // 2, 8, 128), 1) < 4
    first, second = [], []
    for t in range(half):
        both = fin_buf[:, t].astype(F32)
        turned = roll4(both).reshape(nd // 2, 2, 8, 128)
        both = both.reshape(nd // 2, 2, 8, 128)
        first.append(jnp.where(low3, both[:, 0], turned[:, 1]).reshape(nd * 4, 128))
        second.append(jnp.where(low3, turned[:, 0], both[:, 1]).reshape(nd * 4, 128))
    logits = nt(jnp.concatenate(first + second, axis=1).astype(BF16), emb[...])
    peak = jnp.max(logits, axis=1, keepdims=True)
    level = peak + jnp.log(jnp.sum(jnp.exp(logits - peak), axis=1, keepdims=True))
    st1[f] = jnp.transpose(jnp.broadcast_to(level, (nd * 4, 128)))[0:1]
    frames_send(14, st1)
    received(14, st1, NF - 1)

    def joined_levels(levels):
        top = jnp.max(levels, axis=0)
        return top + jnp.log(jnp.sum(jnp.exp(levels - top[None]), axis=0))

    st2[d] = joined_levels(st1[...])
    dp_send(15, st2)
    received(15, st2, nd - 1)
    whole = joined_levels(st2[...])
    out_ref[...] = logits - jnp.transpose(jnp.broadcast_to(whole, (128, nd * 4)))[:, :vocab]

    for n, buf, count in exchanges:
        pltpu.make_async_copy(buf.at[pl.ds(0, count)], buf.at[pl.ds(0, count)], ssem.at[n]).wait()


def on_device(nd, *args):
    (token_ids, positions, embed, pos_table, self_keys, self_values, cross_keys, cross_values, norm_gains, qkv_weight,
     out_weight, cross_query_weight, cross_out_weight, up_weight, down_weight) = args
    vocab = embed.shape[0]
    slots, frames, hidden = self_keys.shape[1], cross_keys.shape[1], up_weight.shape[1]
    streams = nd * 4
    vm = pltpu.VMEM
    big = args[2:]
    held = [vm(a.shape, a.dtype) for a in big]
    scratch = held + [
        vm((3, WIDTH, 256), BF16), vm((WIDTH, 256), BF16), vm((WIDTH, 256), BF16), vm((WIDTH, 256), BF16),
        vm((nd, 8, 128), I32),
        vm((NF, vocab, 256), BF16),
        vm((nd, 8, 128), BF16), vm((nd, 8, 128), BF16),
        vm((NF, 8, 128), BF16),
        vm((NF, 3, 8, 128), BF16),
        vm((NF, TILES // 2, 8, 128), BF16), vm((NF, 8, 128), F32),
        vm((NF, 8, 128), BF16), vm((NF, 8, 128), BF16),
        vm((NF, TILES // 2, 8, 128), BF16), vm((NF, 8, 128), F32),
        vm((NF, 8, 128), BF16),
        vm((NF, TILES // 2, 8, 128), BF16),
        vm((nd, TILES // 2, 8, 128), BF16),
        vm((NF, 1, streams), F32), vm((nd, 1, streams), F32),
        pltpu.SemaphoreType.DMA((len(big),)), pltpu.SemaphoreType.DMA((16,)), pltpu.SemaphoreType.DMA((16,)),
    ]
    return pl.pallas_call(
        functools.partial(kernel, nd, vocab, slots, frames, hidden),
        out_shape=jax.ShapeDtypeStruct((streams, vocab), F32),
        in_specs=[pl.BlockSpec(memory_space=pltpu.SMEM)] * 2 + [pl.BlockSpec(memory_space=pl.ANY)] * len(big),
        out_specs=pl.BlockSpec(memory_space=pltpu.VMEM),
        scratch_shapes=scratch,
        compiler_params=pltpu.CompilerParams(collective_id=0, has_side_effects=True, vmem_limit_bytes=60 * 1024 * 1024),
    )(*args)


def solution(mesh):
    nd = mesh.shape["dp"]
    both = ("dp", "frames")
    in_specs = (
        P("dp"), P("dp"), P(both, None), P(),
        P("dp", "frames", None), P("dp", "frames", None), P("dp", "frames", None), P("dp", "frames", None),
        P(), P(None, None, "frames"), P(None, "frames"), P(None, "frames"), P(None, "frames"), P(None, "frames"),
        P("frames", None),
    )
    return jax.shard_map(functools.partial(on_device, nd), mesh=mesh, in_specs=in_specs, out_specs=P(None, both),
                         check_vma=False)
```

time: 204 us -> 90.1 us (0.44)
  blocking collectives: 86.5 us -> 0 us
  Pallas kernels: 0 us -> 80.7 us
  starting transfers between devices: 37.5 us -> 0 us
  waiting for transfers between devices: 32.6 us -> 0 us
  local copies, waits for them, and re-layouts: 27.8 us -> 9.18 us
  matrix products: 9.54 us -> 0 us
  other arithmetic: 8.54 us -> 0 us
    pallas_call x0 -> x1, Pallas kernels: none -> 80.7 us  [on_device(): pl.pallas_call(functools.partial(kernel, nd, vocab, slots, frames, hidden...]
    all_to_all x5 -> x0, blocking collectives: 49.1 us -> none  [copy_for_each(): lax.all_to_all(jnp.broadcast_to(value[None], (devices, *value.shape)), ax...]
    all_to_all x6 -> x0, starting transfers between devices: 37.5 us -> none  [the longest x5 33.6 us: copy_for_each(): lax.all_to_all(jnp.broadcast_to(value[None], (devices, *value.shape)), ax...]
    all_gather x4 -> x0, blocking collectives: 37.4 us -> none  [collected_together(): both, at, found = (lax.all_gather(jnp.concatenate(lines), axis), 0, {})]
    all_to_all x6 -> x0, waiting for transfers between devices: 32.6 us -> none  [the longest x5 22.7 us: copy_for_each(): lax.all_to_all(jnp.broadcast_to(value[None], (devices, *value.shape)), ax...]
    dot_general x12 -> x0, matrix products: 9.54 us -> none  [the longest x2 2.18 us: partial_attention(): jnp.einsum('she,sche->shc', query, keys4, preferred_element_type=jnp.floa...]
    slice x15 -> x0, local copies, waits for them, and re-layouts: 8.7 us -> none  [the longest x8 5.03 us: folded_in_pairs(): part[side::2]]
    reshape x23 -> x0, local copies, waits for them, and re-layouts: 8.45 us -> none  [the longest x2 3.57 us: partial_attention(): vals4 = values.reshape(streams, slots, HEADS, size)]
  transfers between devices with their start and end apart: 6 -> 0, of which waited for: 6 -> 0; matrix products, arithmetic and copies ran while one was open for 4% -> 0% of each run, Pallas kernels for 0% -> 0%
where the time goes in v1:
time: 90.1 us; the launch traced here: 89.9 us
  Pallas kernels  80.7 us (90%)
  local copies, waits for them, and re-layouts  9.18 us (10%)
    pallas_call x1, Pallas kernels, on_device(): pl.pallas_call(functools.partial(kernel, nd, vocab, slots, frames, hidden...  80.7 us
    unnamed x8, local copies, waits for them, and re-layouts  7.62 us

profile of v1, /device:TPU:1, one launch (start us, length us, event | category | flops | bytes accessed | tf_op | source)
XLA Modules:
  0.0 89.9 jit_solution(15861877290836193036)
XLA Ops:
  0.0 0.0 copy-start.1
  0.0 0.0 copy-start
  0.0 2.2 %copy.17.ow_h = bf16[1280,160]{1,0:T(8,128)(2,1)} copy(bf16[1280,160]{0,1:T(8,128)(2,1)} %param.25) | data formatting | bytes 819200 | tf_op args[10]
  2.2 2.1 %copy.18.cqw_h = bf16[1280,160]{1,0:T(8,128)(2,1)} copy(bf16[1280,160]{0,1:T(8,128)(2,1)} %param.26) | data formatting | bytes 819200 | tf_op args[11]
  4.3 0.0 copy-done.1
  4.3 1.1 %copy.19.cow_h = bf16[1280,160]{1,0:T(8,128)(2,1)} copy(bf16[1280,160]{0,1:T(8,128)(2,1)S(1)} %copy-done.1) | data formatting | bytes 819200 | tf_op args[12]
  5.4 0.0 copy-done
  5.4 2.3 %copy.16.qkv_h = bf16[3,1280,160]{2,1,0:T(8,128)(2,1)} copy(bf16[3,1280,160]{1,2,0:T(8,128)(2,1)S(1)} %copy-done) | data formatting | bytes 2457600 | tf_op args[9]
  7.6 80.7 %shard_map.145 = f32[128,104]{1,0:T(8,128)} custom-call(s32[4]{0:T(128)} %tok_ref.1, s32[4]{0:T(128)} %pos_ref.1, bf16[104,1280]{1,0:T(8,128)(2,1)} %emb_h.1, bf16[256,1280]{1,0:T(8,128)(2,1)} %post_h.1, bf16[4,32,1280]{2,1,0:T(8,128)(2,1)} %sk_h.1, bf16[4,32,1280]{2,1,0:T(8,128)(2,1)} %sv_h.1, bf16[4,64,1280]{2,1,0:T(8,128)(2,1)} %ck_h.1, ...), custom_call_target="tpu_custom_call" | custom-call | tf_op jit(solution)/shard_map/pallas_call | solution.py:359
  88.3 1.6 %copy.20 = f32[128,104]{0,1:T(8,128)} copy(f32[128,104]{1,0:T(8,128)} %shard_map.145) | data formatting | bytes 106496 | tf_op jit(solution)/shard_map/pallas_call | solution.py:359
Async XLA Ops:
  0.0 4.3 %copy-start.1 = (bf16[1280,160]{0,1:T(8,128)(2,1)S(1)}, bf16[1280,160]{0,1:T(8,128)(2,1)}, u32[]{:S(2)}) copy-start(bf16[1280,160]{0,1:T(8,128)(2,1)} %param.27) | copy-start | bytes 1228804
  0.0 5.4 %copy-start = (bf16[3,1280,160]{1,2,0:T(8,128)(2,1)S(1)}, bf16[3,1280,160]{1,2,0:T(8,128)(2,1)}, u32[]{:S(2)}) copy-start(bf16[3,1280,160]{1,2,0:T(8,128)(2,1)} %param.24) | copy-start | bytes 3686404

commit v2 on v1

--- a/solution.py
+++ b/solution.py
@@ -8,6 +8,7 @@
 from jax.sharding import PartitionSpec as P
 
 MESH = pl.DeviceIdType.MESH
+PHASES = False
 F32, BF16, I32 = jnp.float32, jnp.bfloat16, jnp.int32
 HEADS = 20
 WIDTH = 1280
@@ -29,7 +30,7 @@
 def kernel(nd, vocab, slots, frames, hidden,
            tok_ref, pos_ref, emb_h, post_h, sk_h, sv_h, ck_h, cv_h, gain_h, qkv_h, ow_h, cqw_h, cow_h, up_h, down_h,
            out_ref,
-           emb, post, sk, sv, ck, cv, gain, qkvw, ow, cqw, cow, up, down,
+           emb, post, sk, sv, ck, cv, gain, up, down,
            pqkv, pow_, pcq, pco,
            ids_buf, ew, row_send, row_buf, tok_buf, qkv_buf, smix, sstat, so_buf, cq_buf, cmix, cstat, co_buf, dn_buf,
            fin_buf, st1, st2,
@@ -41,11 +42,25 @@
     low = sub < 4
     own_half = (sub // 4) == (lane // 64)
 
+    scopes = []
+
+    def phase(name):
+        if PHASES:
+            if scopes:
+                scopes.pop().__exit__(None, None, None)
+            if name:
+                scopes.append(jax.named_scope(name))
+                scopes[0].__enter__()
+
+    phase("load")
+
     def roll4(v):
         return pltpu.roll(v, 4, v.ndim - 2)
 
-    pairs = [(emb_h, emb), (post_h, post), (qkv_h, qkvw), (gain_h, gain), (sk_h, sk), (sv_h, sv), (ow_h, ow),
-             (cqw_h, cqw), (ck_h, ck), (cv_h, cv), (cow_h, cow), (up_h, up), (down_h, down)]
+    window = pl.ds(pl.multiple_of(lax.rem(f, 4) * 32, 32), PIECE)
+    pairs = [(emb_h, emb), (post_h, post), (qkv_h, pqkv.at[:, window, :]), (gain_h, gain), (sk_h, sk), (sv_h, sv),
+             (ow_h, pow_.at[window, :]), (cqw_h, pcq.at[window, :]), (ck_h, ck), (cv_h, cv), (cow_h, pco.at[window, :]),
+             (up_h, up), (down_h, down)]
     local = {}
     for n, (src, dst) in enumerate(pairs):
         local[n] = pltpu.make_async_copy(src, dst, lsem.at[n])
@@ -84,7 +99,9 @@
         return jnp.where(index == 0, a, jnp.where(index == 1, b, jnp.where(index == 2, c, e)))
 
     ids_buf[d] = by_stream(sub % 4, t0, t1, t2, t3)
+    phase("barrier")
     pl.semaphore_wait(barrier, nd - 1 + NF - 1)
+    phase("ids_send")
     dp_send(0, ids_buf)
 
     def first_lane(index):
@@ -99,27 +116,23 @@
     exchanges.append((1, ew, NF - 1))
     ew[f] = emb[:, pl.ds(first_lane(f), 256)]
 
+    phase("idle_work")
     local[POST].wait()
     places = post.shape[0]
     place_at = by_stream(lax.broadcasted_iota(I32, (8, places), 0) % 4, p0, p1, p2, p3)
     place_hit = (lax.broadcasted_iota(I32, (8, places), 1) == place_at).astype(F32).astype(BF16)
     place = nn(place_hit, post[...])
 
-    shift = lax.rem(f, 4) * 32
-    move = (lax.broadcasted_iota(I32, (PIECE, 256), 1)
-            == lax.broadcasted_iota(I32, (PIECE, 256), 0) + shift).astype(F32).astype(BF16)
-    local[QKV].wait()
-    for j in range(3):
-        pqkv[j] = nn(qkvw[j], move).astype(BF16)
-    local[OW].wait()
-    pow_[...] = nn(ow[...], move).astype(BF16)
-    local[CQW].wait()
-    pcq[...] = nn(cqw[...], move).astype(BF16)
-    local[COW].wait()
-    pco[...] = nn(cow[...], move).astype(BF16)
-
+    for i in range(3):
+        rest = pl.ds(pl.multiple_of(lax.rem(lax.rem(f, 4) + 5 + i, 8) * 32, 32), 32)
+        pqkv[:, rest, :] = jnp.zeros((3, 32, WIDTH), BF16)
+        for ref in (pow_, pcq, pco):
+            ref[rest, :] = jnp.zeros((32, WIDTH), BF16)
+
+    phase("ids_wait")
     received(1, ew, NF - 1)
     received(0, ids_buf, nd - 1)
+    phase("onehot")
     ids = ids_buf[...].reshape(nd * 8, 128)[:, :vocab]
     row_of = lax.broadcasted_iota(I32, (nd * 8, vocab), 1)
     found = None
@@ -130,19 +143,24 @@
     low_rows = (lax.broadcasted_iota(I32, (nd * 8, 128), 0) % 8) < 4
     folded = jnp.where(low_rows, found[:, :128], found[:, 128:])
     row_send[...] = folded.reshape(nd, 8, 128).astype(BF16)
+    phase("rows_send")
     for k in range(1, nd):
         peer = lax.rem(d + k, nd)
         pltpu.make_async_remote_copy(
             src_ref=row_send.at[peer], dst_ref=row_buf.at[d], send_sem=ssem.at[2], recv_sem=rsem.at[2],
             device_id=(peer, f), device_id_type=MESH).start()
     exchanges.append((2, row_buf, nd - 1))
+    phase("rows_wait")
     row_buf[d] = row_send[d]
     received(2, row_buf, nd - 1)
+    phase("rows_sum")
     tok_buf[f] = jnp.sum(row_buf[...].astype(F32), axis=0).astype(BF16)
+    phase("tok_x")
     frames_send(3, tok_buf)
     local[GAIN].wait()
     received(3, tok_buf, NF - 1)
 
+    phase("ln1")
     def unfold(v):
         other = roll4(v)
         return jnp.where(low, v, other), jnp.where(low, other, v)
@@ -172,7 +190,10 @@
         return tiles
 
     normed = norm(start, 0)
-    qkv_buf[f] = jnp.stack([fold_window(nn(normed, pqkv[j])) for j in range(3)])
+    local[QKV].wait()
+    phase("qkv_mm")
+    qkv_buf[f] = jnp.stack([fold_window(nt(normed, pqkv[j])) for j in range(3)])
+    phase("qkv_x")
     frames_send(4, qkv_buf)
 
     rows_r = 4 * HEADS
@@ -245,6 +266,7 @@
     local[SK].wait()
     local[SV].wait()
     received(4, qkv_buf, NF - 1)
+    phase("attn1")
     query, key_new, value_new = (columns_joined([qkv_buf[k, j] for k in range(NF)]) for j in range(3))
     first_device = f == 0
     own_scores = []
@@ -252,34 +274,47 @@
         score = jnp.sum(jnp.where(own_half, query[t] * key_new[t], 0.0), axis=1, keepdims=True) * 0.125
         own_scores.append(jnp.where(first_device, score, NEG))
     smix[f], sstat[f] = attend(query, sk, sv, slots, valid, (own_scores, value_new))
+    phase("mix1_x")
     frames_send(5, sstat)
     frames_send(6, smix)
     received(5, sstat, NF - 1)
     received(6, smix, NF - 1)
+    phase("join1")
     self_mix = joined(smix, sstat)
 
-    so_buf[f] = fold_window(nn(self_mix, pow_[...]))
+    local[OW].wait()
+    so_buf[f] = fold_window(nt(self_mix, pow_[...]))
+    phase("so_x")
     frames_send(7, so_buf)
     received(7, so_buf, NF - 1)
+    phase("ln2")
     after_self = start + jnp.concatenate(columns_joined([so_buf[k] for k in range(NF)]), axis=1)
     normed2 = norm(after_self, 1)
-    cq_buf[f] = fold_window(nn(normed2, pcq[...]))
+    local[CQW].wait()
+    cq_buf[f] = fold_window(nt(normed2, pcq[...]))
+    phase("cq_x")
     frames_send(8, cq_buf)
     local[CK].wait()
     local[CV].wait()
     received(8, cq_buf, NF - 1)
+    phase("attn2")
     cross_query = columns_joined([cq_buf[k] for k in range(NF)])
     cmix[f], cstat[f] = attend(cross_query, ck, cv, frames, every, None)
+    phase("mix2_x")
     frames_send(9, cstat)
     frames_send(10, cmix)
     received(9, cstat, NF - 1)
     received(10, cmix, NF - 1)
+    phase("join2")
     cross_mix = joined(cmix, cstat)
-    co_buf[f] = fold_window(nn(cross_mix, pco[...]))
+    local[COW].wait()
+    co_buf[f] = fold_window(nt(cross_mix, pco[...]))
+    phase("co_x")
     frames_send(11, co_buf)
     local[UP].wait()
     local[DOWN].wait()
     received(11, co_buf, NF - 1)
+    phase("mlp")
     after_cross = after_self + jnp.concatenate(columns_joined([co_buf[k] for k in range(NF)]), axis=1)
 
     normed3 = norm(after_cross, 2)
@@ -292,16 +327,20 @@
         return v[:, 128 * t : 128 * t + 128]
 
     dn_buf[f] = jnp.stack([jnp.where(low, tile(lowered, t), tile(lowered, t + half)).astype(BF16) for t in range(half)])
+    phase("dn_x")
     frames_send(12, dn_buf)
     received(12, dn_buf, NF - 1)
+    phase("ln4")
     summed = jnp.sum(dn_buf[...].astype(F32), axis=0)
     halves = [unfold(summed[t]) for t in range(half)]
     after_mlp = after_cross + jnp.concatenate([a for a, _ in halves] + [b for _, b in halves], axis=1)
     final = norm(after_mlp, 3).astype(F32)
     fin_buf[d] = jnp.stack([jnp.where(low, tile(final, t), tile(final, t + half)).astype(BF16) for t in range(half)])
+    phase("fin_x")
     dp_send(13, fin_buf)
     received(13, fin_buf, nd - 1)
 
+    phase("logits")
     low3 = lax.broadcasted_iota(I32, (nd // 2, 8, 128), 1) < 4
     first, second = [], []
     for t in range(half):
@@ -310,10 +349,10 @@
         both = both.reshape(nd // 2, 2, 8, 128)
         first.append(jnp.where(low3, both[:, 0], turned[:, 1]).reshape(nd * 4, 128))
         second.append(jnp.where(low3, turned[:, 0], both[:, 1]).reshape(nd * 4, 128))
-    logits = nt(jnp.concatenate(first + second, axis=1).astype(BF16), emb[...])
-    peak = jnp.max(logits, axis=1, keepdims=True)
-    level = peak + jnp.log(jnp.sum(jnp.exp(logits - peak), axis=1, keepdims=True))
-    st1[f] = jnp.transpose(jnp.broadcast_to(level, (nd * 4, 128)))[0:1]
+    logits = nt(emb[...], jnp.concatenate(first + second, axis=1).astype(BF16))
+    peak = jnp.max(logits, axis=0, keepdims=True)
+    st1[f] = peak + jnp.log(jnp.sum(jnp.exp(logits - peak), axis=0, keepdims=True))
+    phase("stats_frames")
     frames_send(14, st1)
     received(14, st1, NF - 1)
 
@@ -322,13 +361,16 @@
         return top + jnp.log(jnp.sum(jnp.exp(levels - top[None]), axis=0))
 
     st2[d] = joined_levels(st1[...])
+    phase("stats_dp")
     dp_send(15, st2)
     received(15, st2, nd - 1)
-    whole = joined_levels(st2[...])
-    out_ref[...] = logits - jnp.transpose(jnp.broadcast_to(whole, (128, nd * 4)))[:, :vocab]
-
+    phase("out")
+    out_ref[...] = logits - joined_levels(st2[...])
+
+    phase("drain")
     for n, buf, count in exchanges:
         pltpu.make_async_copy(buf.at[pl.ds(0, count)], buf.at[pl.ds(0, count)], ssem.at[n]).wait()
+    phase(None)
 
 
 def on_device(nd, *args):
@@ -338,10 +380,12 @@
     slots, frames, hidden = self_keys.shape[1], cross_keys.shape[1], up_weight.shape[1]
     streams = nd * 4
     vm = pltpu.VMEM
-    big = args[2:]
-    held = [vm(a.shape, a.dtype) for a in big]
+    big = (embed, pos_table, self_keys, self_values, cross_keys, cross_values, norm_gains, jnp.swapaxes(qkv_weight, 1, 2),
+           out_weight.T, cross_query_weight.T, cross_out_weight.T, up_weight, down_weight)
+    held = [vm(a.shape, a.dtype) for a in (embed, pos_table, self_keys, self_values, cross_keys, cross_values, norm_gains,
+                                           up_weight, down_weight)]
     scratch = held + [
-        vm((3, WIDTH, 256), BF16), vm((WIDTH, 256), BF16), vm((WIDTH, 256), BF16), vm((WIDTH, 256), BF16),
+        vm((3, 256, WIDTH), BF16), vm((256, WIDTH), BF16), vm((256, WIDTH), BF16), vm((256, WIDTH), BF16),
         vm((nd, 8, 128), I32),
         vm((NF, vocab, 256), BF16),
         vm((nd, 8, 128), BF16), vm((nd, 8, 128), BF16),
@@ -358,12 +402,12 @@
     ]
     return pl.pallas_call(
         functools.partial(kernel, nd, vocab, slots, frames, hidden),
-        out_shape=jax.ShapeDtypeStruct((streams, vocab), F32),
+        out_shape=jax.ShapeDtypeStruct((vocab, streams), F32),
         in_specs=[pl.BlockSpec(memory_space=pltpu.SMEM)] * 2 + [pl.BlockSpec(memory_space=pl.ANY)] * len(big),
         out_specs=pl.BlockSpec(memory_space=pltpu.VMEM),
         scratch_shapes=scratch,
         compiler_params=pltpu.CompilerParams(collective_id=0, has_side_effects=True, vmem_limit_bytes=60 * 1024 * 1024),
-    )(*args)
+    )(token_ids, positions, *big).T
 
 
 def solution(mesh):

time: 90.1 us -> 83 us (0.921)
  local copies, waits for them, and re-layouts: 9.18 us -> 1.43 us
    unnamed x8 -> x1, local copies, waits for them, and re-layouts: 7.62 us -> 1.43 us
    pallas_call x1 -> x0, local copies, waits for them, and re-layouts: 1.55 us -> none  [on_device(): pl.pallas_call(functools.partial(kernel, nd, vocab, slots, frames, hidden...]
where the time goes in v2:
time: 83 us; the launch traced here: 82.9 us
  Pallas kernels  81.4 us (98%)
  local copies, waits for them, and re-layouts  1.43 us (2%)
    pallas_call x1, Pallas kernels, on_device(): pl.pallas_call(functools.partial(kernel, nd, vocab, slots, frames, hidden...  81.4 us

profile of v2, /device:TPU:1, one launch (start us, length us, event | category | flops | bytes accessed | tf_op | source)
XLA Modules:
  0.0 82.9 jit_solution(16919951264189911985)
XLA Ops:
  0.0 81.4 %shard_map.145 = f32[104,128]{1,0:T(8,128)} custom-call(s32[4]{0:T(128)} %tok_ref.1, s32[4]{0:T(128)} %pos_ref.1, bf16[104,1280]{1,0:T(8,128)(2,1)} %emb_h.1, bf16[256,1280]{1,0:T(8,128)(2,1)} %post_h.1, bf16[4,32,1280]{2,1,0:T(8,128)(2,1)} %sk_h.1, bf16[4,32,1280]{2,1,0:T(8,128)(2,1)} %sv_h.1, bf16[4,64,1280]{2,1,0:T(8,128)(2,1)} %ck_h.1, ...), custom_call_target="tpu_custom_call" | custom-call | tf_op jit(solution)/shard_map/pallas_call | solution.py:403
  81.4 1.4 %copy.17 = f32[128,104]{0,1:T(8,128)} copy(f32[128,104]{0,1:T(8,128)} %bitcast.9) | data formatting | bytes 106496
